TPU v7x, 32 devices: a whole 2x2x4 slice. The times are simulated.
32 devices in a mesh: grp: 2 (over x), blk: 16 (over z, y, core).
Axes of the slice: x: 2, y: 2, z: 4, core: 2. Of those that a mesh axis runs over, the one named last changes fastest.
Arguments:
- atoms: bfloat16 [16384, 512], P(('grp', 'blk')), parts along dimension 0, may hold values from -8 to 8
- edge_mask: int32 [32, 5, 512, 512], P(('grp', 'blk')), parts along dimension 0, may hold values from 0 to 1
- norm_gain: float32 [512], replicated, may hold values from 0.25 to 1.75
- w_query: bfloat16 [512, 512], replicated, may hold values from -3 to 3
- w_key: bfloat16 [512, 512], replicated, may hold values from -3 to 3
- w_value: bfloat16 [512, 512], replicated, may hold values from -0.25 to 0.25
- w_out: bfloat16 [512, 512], replicated, may hold values from -0.25 to 0.25
- bn_gain: float32 [512], replicated, may hold values from 0.25 to 1.75
- bn_shift: float32 [512], replicated, may hold values from -3 to 3
- w_up: bfloat16 [512, 1024], replicated, may hold values from -0.25 to 0.25
- w_down: bfloat16 [1024, 512], replicated, may hold values from -0.1875 to 0.1875
Outputs:
- updated: bfloat16 [16384, 512], P(('grp', 'blk')), parts along dimension 0
There are 2 independent parts, one for each index of `grp`. A program takes and returns all parts, laid end to end along the dimension named above; an argument that names none is the same for every part. Nothing has to cross between parts.
All inputs are finite; a program needn't handle non-finite values.
Results may differ from a plain program's by a relative error of at most 0.01.
The roundings to bfloat16 on the way count: a program that leaves them out, or rounds other values in their place, can miss the bound.
Values may be sent and summed in bfloat16 or wider, within the bound.
A program may use at most 128 MiB of HBM per device.

v0:
```python
import functools

import jax
import jax.numpy as jnp
from jax import lax
from jax.experimental import pallas as pl
from jax.experimental.pallas import tpu as pltpu
from jax.sharding import PartitionSpec as P

HEAD_DIM = 64
PAIR = 2 * HEAD_DIM
REACH = 2
CHUNKS = 4
NEG = -1e30
MESH = pl.DeviceIdType.MESH
PARTNER, MIRROR, RAIL, CROSS = 0, 1, 2, 3
ROWS_STEP = 128
UNROLL = 2
SLOTS = 2


def kernel(
    n,
    atoms_hbm, mask_hbm, ng_hbm, wq_hbm, wk_hbm, wv_hbm, wo_hbm, bg_hbm, bs_hbm, wu_hbm, wd_hbm,
    out_ref,
    x_ref, mask_ref, ng_ref, wq_ref, wk_ref, wv_ref, wo_ref, bg_ref, bs_ref, wu_ref, wd_ref,
    nb_ref, qm_ref, kb_ref, va_ref, bias_ref, m_ref, l_ref, acc_ref, mixed_ref, after_ref,
    stats_ref, load_sem, mask_sem,
    p_send, p_recv, m_send, m_recv, r_send, r_recv, c_send, c_recv, s_send, s_recv,
):
    me = lax.axis_index("blk")
    rows, width = x_ref.shape
    pairs = width // PAIR
    group, inside = me // 4, me % 4
    side, core = inside // 2, inside % 2
    partner = group * 4 + side * 2 + (1 - core)
    mirror = group * 4 + (1 - side) * 2 + core
    groups = n // 4
    rail_to = ((group + 1 - 2 * side + groups) % groups) * 4 + side * 2 + core
    cross_source = jnp.where(side == core, MIRROR, RAIL)

    barrier = pltpu.get_barrier_semaphore()

    def greet(d, carry):
        pl.semaphore_signal(
            barrier, inc=1, device_id={"blk": lax.rem(me + d, n)}, device_id_type=MESH
        )
        return carry

    lax.fori_loop(1, n, greet, 0)

    sources = (
        (atoms_hbm, x_ref), (ng_hbm, ng_ref), (wq_hbm, wq_ref), (wk_hbm, wk_ref), (wv_hbm, wv_ref),
        (wo_hbm, wo_ref), (bg_hbm, bg_ref), (bs_hbm, bs_ref), (wu_hbm, wu_ref), (wd_hbm, wd_ref),
    )
    loads = [
        pltpu.make_async_copy(src, dst, load_sem.at[i]) for i, (src, dst) in enumerate(sources)
    ]

    far = jnp.where(side == 0, 2, -2)
    near = jnp.where(core == 0, 1, -1)
    offsets = [jnp.int32(0), near, far, -far, -near]
    masks = [
        pltpu.make_async_copy(
            mask_hbm.at[0, offsets[i] + REACH], mask_ref.at[i], mask_sem.at[i]
        )
        for i in range(2 * REACH + 1)
    ]
    for i in range(5):
        loads[i].start()
    for mask_load in masks:
        mask_load.start()
    for i in range(5, len(loads)):
        loads[i].start()

    step_rows = rows // CHUNKS

    def chunk(c):
        return pl.ds(c * step_rows, step_rows)

    def mirror_copy(c):
        return pltpu.make_async_remote_copy(
            src_ref=x_ref.at[chunk(c)], dst_ref=nb_ref.at[MIRROR, chunk(c)],
            send_sem=m_send.at[c], recv_sem=m_recv.at[c],
            device_id={"blk": mirror}, device_id_type=MESH,
        )

    def rail_copy(c):
        return pltpu.make_async_remote_copy(
            src_ref=nb_ref.at[MIRROR, chunk(c)], dst_ref=nb_ref.at[RAIL, chunk(c)],
            send_sem=r_send.at[c], recv_sem=r_recv.at[c],
            device_id={"blk": rail_to}, device_id_type=MESH,
        )

    def cross_copy(c):
        return pltpu.make_async_remote_copy(
            src_ref=nb_ref.at[cross_source, chunk(c)], dst_ref=nb_ref.at[CROSS, chunk(c)],
            send_sem=c_send.at[c], recv_sem=c_recv.at[c],
            device_id={"blk": partner}, device_id_type=MESH,
        )

    partner_copy = pltpu.make_async_remote_copy(
        src_ref=x_ref, dst_ref=nb_ref.at[PARTNER], send_sem=p_send, recv_sem=p_recv,
        device_id={"blk": partner}, device_id_type=MESH,
    )

    def relay_rail(c):
        mirror_copy(c).wait_recv()
        rail_copy(c).start()

    def relay_cross(c):
        rail_copy(c).wait_recv()
        cross_copy(c).start()

    def normalize(value):
        full = value.astype(jnp.float32)
        return (
            full * lax.rsqrt(jnp.mean(full * full, axis=-1, keepdims=True) + 1e-06) * ng_ref[...]
        ).astype(jnp.bfloat16)

    left = lax.broadcasted_iota(jnp.int32, (rows, PAIR), 1) < HEAD_DIM
    left_step = lax.broadcasted_iota(jnp.int32, (ROWS_STEP, PAIR), 1) < HEAD_DIM
    pieces = rows // ROWS_STEP

    for g in range(SLOTS):
        for h in range(pairs):
            va_ref[g, h, :, PAIR:] = jnp.ones((rows, PAIR), jnp.bfloat16)

    def set_keys(g, normed):
        keys = jnp.dot(normed, wk_ref[...], preferred_element_type=jnp.float32).astype(jnp.bfloat16)
        values = jnp.dot(normed, wv_ref[...], preferred_element_type=jnp.float32).astype(jnp.bfloat16)
        for h in range(pairs):
            kb_ref[g, h] = keys[:, h * PAIR:(h + 1) * PAIR]
            va_ref[g, h, :, :PAIR] = values[:, h * PAIR:(h + 1) * PAIR]

    def set_bias(g, i):
        masks[i].wait()
        allowed = mask_ref[i] > 0
        if i == 0:
            allowed = allowed | (
                lax.broadcasted_iota(jnp.int32, (rows, rows), 0)
                == lax.broadcasted_iota(jnp.int32, (rows, rows), 1)
            )
        bias_ref[g] = jnp.where(allowed, 0.0, NEG)

    def attend(count, first, between):
        blocks = rows // PAIR

        def scores(h, r):
            piece = pl.ds(r * ROWS_STEP, ROWS_STEP)
            found = []
            peaks = [None, None]
            for g in range(count):
                score = lax.dot_general(
                    qm_ref[h, r], kb_ref[g, h], (((1,), (1,)), ((), ())),
                    preferred_element_type=jnp.float32,
                )
                for b in range(blocks):
                    bias = bias_ref[g, piece, b * PAIR:(b + 1) * PAIR]
                    both = []
                    for j in range(2):
                        part = score[
                            j * ROWS_STEP:(j + 1) * ROWS_STEP, b * PAIR:(b + 1) * PAIR
                        ] + bias
                        peaks[j] = part if peaks[j] is None else jnp.maximum(peaks[j], part)
                        both.append(part)
                    found.append(both)
            return found, peaks

        def finish(h, r, found, peaks):
            piece = pl.ds(r * ROWS_STEP, ROWS_STEP)
            if not first:
                old = m_ref[h, piece]
                peaks = [
                    jnp.maximum(peaks[0], jnp.where(left_step, old, NEG)),
                    jnp.maximum(peaks[1], jnp.where(left_step, NEG, old)),
                ]
            tops = [
                jnp.broadcast_to(jnp.max(peak, axis=-1, keepdims=True), (ROWS_STEP, PAIR))
                for peak in peaks
            ]
            new = jnp.where(left_step, tops[0], tops[1])
            m_ref[h, piece] = new
            result = None
            for g in range(count):
                weight = jnp.concatenate([
                    jnp.concatenate([
                        jnp.exp(found[g * blocks + b][j] - tops[j]).astype(jnp.bfloat16)
                        for b in range(blocks)
                    ], axis=1)
                    for j in range(2)
                ], axis=0)
                product = jnp.dot(weight, va_ref[g, h], preferred_element_type=jnp.float32)
                result = product if result is None else result + product
            mixed = jnp.where(left_step, result[:ROWS_STEP, :PAIR], result[ROWS_STEP:, :PAIR])
            total = jnp.where(left_step, result[:ROWS_STEP, PAIR:], result[ROWS_STEP:, PAIR:])
            if first:
                acc_ref[h, piece] = mixed
                l_ref[h, piece] = total
            else:
                factor = jnp.exp(old - new)
                acc_ref[h, piece] = acc_ref[h, piece] * factor + mixed
                l_ref[h, piece] = l_ref[h, piece] * factor + total

        def some_pairs(t, carry):
            units = [(t * UNROLL + u, r) for u in range(UNROLL) for r in range(pieces)]
            ahead = scores(*units[0])
            for k, unit in enumerate(units):
                current = ahead
                if k + 1 < len(units):
                    ahead = scores(*units[k + 1])
                finish(*unit, *current)
            between(t)
            return carry

        lax.fori_loop(0, pairs // UNROLL, some_pairs, 0)

    half = CHUNKS // 2

    def each(relay, base):
        def run(t):
            for u in range(UNROLL):
                h = t * UNROLL + u
                @pl.when(lax.rem(h, 2) == 1)
                def _():
                    relay(base + h // 2)
        return run

    def nothing(t):
        pass

    loads[0].wait()
    loads[1].wait()
    normed = normalize(x_ref[...])
    loads[2].wait()
    query = jnp.dot(normed, wq_ref[...], preferred_element_type=jnp.float32).astype(jnp.bfloat16)
    query = query * jnp.bfloat16(HEAD_DIM ** (-0.5))
    zero = jnp.zeros((rows, PAIR), jnp.bfloat16)
    for h in range(pairs):
        piece = query[:, h * PAIR:(h + 1) * PAIR]
        first_head = jnp.where(left, piece, zero)
        second_head = jnp.where(left, zero, piece)
        for r in range(pieces):
            qm_ref[h, r, :ROWS_STEP] = first_head[r * ROWS_STEP:(r + 1) * ROWS_STEP]
            qm_ref[h, r, ROWS_STEP:] = second_head[r * ROWS_STEP:(r + 1) * ROWS_STEP]
    loads[3].wait()
    loads[4].wait()
    set_keys(0, normed)
    pl.semaphore_wait(barrier, n - 1)
    partner_copy.start()
    for c in range(CHUNKS):
        mirror_copy(c).start()
    set_bias(0, 0)
    attend(1, True, each(relay_rail, 0))

    partner_copy.wait_recv()
    set_keys(0, normalize(nb_ref[PARTNER]))
    set_bias(0, 1)
    attend(1, False, each(relay_rail, half))

    set_keys(0, normalize(nb_ref[MIRROR]))
    set_bias(0, 2)
    attend(1, False, each(relay_cross, 0))

    for c in range(half, CHUNKS):
        relay_cross(c)
    set_keys(0, normalize(nb_ref[RAIL]))
    set_bias(0, 3)
    for c in range(CHUNKS):
        cross_copy(c).wait_recv()
    set_keys(1, normalize(nb_ref[CROSS]))
    set_bias(1, 4)
    attend(2, False, nothing)

    for h in range(pairs):
        mixed_ref[:, h * PAIR:(h + 1) * PAIR] = (acc_ref[h] / l_ref[h]).astype(jnp.bfloat16)
    for load in loads[5:]:
        load.wait()
    after_ref[...] = x_ref[...].astype(jnp.float32) + jnp.dot(
        mixed_ref[...], wo_ref[...], preferred_element_type=jnp.float32
    )

    local_mean = jnp.sum(after_ref[...], axis=0, keepdims=True) * (1.0 / rows)
    spread = after_ref[...] - local_mean
    stats_ref[0, 0:1] = local_mean
    stats_ref[0, 1:2] = jnp.sum(spread * spread, axis=0, keepdims=True)

    def stats_copy(d):
        return pltpu.make_async_remote_copy(
            src_ref=stats_ref.at[0], dst_ref=stats_ref.at[d],
            send_sem=s_send.at[d], recv_sem=s_recv.at[d],
            device_id={"blk": lax.rem(me + d, n)}, device_id_type=MESH,
        )

    def send_stats(d, carry):
        stats_copy(d).start()
        return carry

    def take_stats(d, carry):
        stats_copy(d).wait_recv()
        return carry

    lax.fori_loop(1, n, send_stats, 0)

    partner_copy.wait_send()
    for c in range(CHUNKS):
        mirror_copy(c).wait_send()
        rail_copy(c).wait_send()
        cross_copy(c).wait_send()

    lax.fori_loop(1, n, take_stats, 0)
    gathered = stats_ref[...]
    means = gathered[:, 0, :]
    mean = jnp.sum(means, axis=0, keepdims=True) * (1.0 / n)
    shifts = means - mean
    var = (
        jnp.sum(gathered[:, 1, :], axis=0, keepdims=True) * (1.0 / rows)
        + jnp.sum(shifts * shifts, axis=0, keepdims=True)
    ) * (1.0 / n)
    gain = lax.rsqrt(var + 1e-05) * bg_ref[...]
    batched = ((after_ref[...] - mean) * gain + bs_ref[...]).astype(jnp.bfloat16)
    hidden = jax.nn.gelu(
        jnp.dot(batched, wu_ref[...], preferred_element_type=jnp.float32), approximate=True
    ).astype(jnp.bfloat16)
    out_ref[...] = (
        after_ref[...] + jnp.dot(hidden, wd_ref[...], preferred_element_type=jnp.float32)
    ).astype(jnp.bfloat16)

    def sent_stats(d, carry):
        stats_copy(d).wait_send()
        return carry

    lax.fori_loop(1, n, sent_stats, 0)


def body(
    atoms, edge_mask, norm_gain, w_query, w_key, w_value, w_out, bn_gain, bn_shift, w_up, w_down
):
    n = lax.axis_size("blk")
    rows, width = atoms.shape
    ff = w_up.shape[1]
    slabs = edge_mask.shape[1]
    pairs = width // PAIR
    bf16, f32 = jnp.bfloat16, jnp.float32
    dma = pltpu.SemaphoreType.DMA
    return pl.pallas_call(
        functools.partial(kernel, n),
        out_shape=jax.ShapeDtypeStruct((rows, width), bf16),
        in_specs=[pl.BlockSpec(memory_space=pl.ANY)] * 11,
        out_specs=pl.BlockSpec(memory_space=pltpu.VMEM),
        scratch_shapes=[
            pltpu.VMEM((rows, width), bf16),
            pltpu.VMEM((slabs, rows, rows), jnp.int32),
            pltpu.VMEM((1, width), f32),
            pltpu.VMEM((width, width), bf16),
            pltpu.VMEM((width, width), bf16),
            pltpu.VMEM((width, width), bf16),
            pltpu.VMEM((width, width), bf16),
            pltpu.VMEM((1, width), f32),
            pltpu.VMEM((1, width), f32),
            pltpu.VMEM((width, ff), bf16),
            pltpu.VMEM((ff, width), bf16),
            pltpu.VMEM((4, rows, width), bf16),
            pltpu.VMEM((pairs, rows // ROWS_STEP, 2 * ROWS_STEP, PAIR), bf16),
            pltpu.VMEM((SLOTS, pairs, rows, PAIR), bf16),
            pltpu.VMEM((SLOTS, pairs, rows, 2 * PAIR), bf16),
            pltpu.VMEM((SLOTS, rows, rows), f32),
            pltpu.VMEM((pairs, rows, PAIR), f32),
            pltpu.VMEM((pairs, rows, PAIR), f32),
            pltpu.VMEM((pairs, rows, PAIR), f32),
            pltpu.VMEM((rows, width), bf16),
            pltpu.VMEM((rows, width), f32),
            pltpu.VMEM((n, 2, width), f32),
            dma((10,)),
            dma((slabs,)),
            dma, dma,
            dma((CHUNKS,)), dma((CHUNKS,)),
            dma((CHUNKS,)), dma((CHUNKS,)),
            dma((CHUNKS,)), dma((CHUNKS,)),
            dma((n,)), dma((n,)),
        ],
        compiler_params=pltpu.CompilerParams(
            collective_id=0, has_side_effects=True, vmem_limit_bytes=60 * 1024 * 1024
        ),
    )(
        atoms, edge_mask, norm_gain.reshape(1, width), w_query, w_key, w_value, w_out,
        bn_gain.reshape(1, width), bn_shift.reshape(1, width), w_up, w_down,
    )


def solution(mesh):
    placed = (
        P(("grp", "blk"), None),
        P(("grp", "blk"), None, None, None),
        P(), P(), P(), P(), P(), P(), P(), P(), P(),
    )
    return jax.shard_map(
        body, mesh=mesh, in_specs=placed, out_specs=P(("grp", "blk"), None), check_vma=False
    )
```

profile of v0, /device:TPU:0, one launch (start us, length us, event | category | flops | bytes accessed | tf_op | source)
XLA Modules:
  0.0 42.6 jit_solution(14682439856146071902)
XLA Ops:
  0.0 40.7 %shard_map.109 = bf16[512,512]{1,0:T(8,128)(2,1)} custom-call(bf16[512,512]{1,0:T(8,128)(2,1)} %atoms_hbm.1, s32[1,5,512,512]{3,2,1,0:T(8,128)} %mask_hbm.1, f32[1,512]{1,0:T(1,128)} %bitcast.3, bf16[512,512]{1,0:T(8,128)(2,1)} %wq_hbm.1, bf16[512,512]{1,0:T(8,128)(2,1)} %wk_hbm.1, bf16[512,512]{1,0:T(8,128)(2,1)} %wv_hbm.1, bf16[512,512]{1,0:T(8,128)(2,1)} %wo_hbm.1, ...), custom_call_target="tpu_custom_call" | custom-call | tf_op jit(solution)/shard_map/pallas_call | solution.py:346
  40.7 1.9 %copy.13 = bf16[512,512]{1,0:T(8,128)(2,1)} copy(bf16[512,512]{1,0:T(8,128)(2,1)} %shard_map.109) | data formatting | bytes 1048576
where the time goes:
time: 42.7 us; the launch traced here: 42.6 us
  Pallas kernels  40.7 us (95%)
  local copies, waits for them, and re-layouts  1.87 us (4%)
    pallas_call x1, Pallas kernels, body(): pl.pallas_call(functools.partial(kernel, n), out_shape=jax.ShapeDtypeStru...  40.7 us
    unnamed x1, local copies, waits for them, and re-layouts  1.87 us

commit v1 on v0

v1 whole, which is shorter than its diff:
```python
import functools
import math

import jax
import jax.numpy as jnp
from jax import lax
from jax.experimental import pallas as pl
from jax.experimental.pallas import tpu as pltpu
from jax.sharding import PartitionSpec as P

HEAD_DIM = 64
PAIR = 2 * HEAD_DIM
REACH = 2
CHUNKS = 8
PARTS = 4
SUMS = 16
NEG = -1e30
MESH = pl.DeviceIdType.MESH
OWN, PARTNER, MIRROR, RAIL, CROSS = 0, 1, 2, 3, 4
SCALE = math.log2(math.e) * HEAD_DIM ** (-0.5)


def kernel(
    n,
    atoms_hbm, mask_hbm, ng_hbm, wq_hbm, wk_hbm, wv_hbm, wo_hbm, bg_hbm, bs_hbm, wu_hbm, wd_hbm,
    out_ref,
    slab_ref, mask_ref, ng_ref, wq_ref, wk_ref, wv_ref, wo_ref, bg_ref, bs_ref, wu_ref, wd_ref,
    wvt_ref, qt_ref, kb_ref, vt_ref, bias_ref, m_ref, acc_ref, mixed_ref, after_ref,
    stats_ref, load_sem, mask_sem,
    p_send, m_send, r_send, c_send, recv, s_send, s_recv,
):
    me = lax.axis_index("blk")
    rows, width = after_ref.shape
    heads = width // HEAD_DIM
    group, inside = me // 4, me % 4
    side, core = inside // 2, inside % 2
    partner = group * 4 + side * 2 + (1 - core)
    mirror = group * 4 + (1 - side) * 2 + core
    groups = n // 4
    rail_to = ((group + 1 - 2 * side + groups) % groups) * 4 + side * 2 + core
    same = side == core
    late_one = jnp.where(same, RAIL, CROSS)
    late_two = jnp.where(same, CROSS, RAIL)

    barrier = pltpu.get_barrier_semaphore()

    def greet(d, carry):
        pl.semaphore_signal(
            barrier, inc=1, device_id={"blk": lax.rem(me + d, n)}, device_id_type=MESH
        )
        return carry

    lax.fori_loop(1, n, greet, 0)

    sources = (
        (atoms_hbm, slab_ref.at[OWN]), (ng_hbm, ng_ref), (wq_hbm, wq_ref), (wk_hbm, wk_ref),
        (wv_hbm, wv_ref), (wo_hbm, wo_ref), (bg_hbm, bg_ref), (bs_hbm, bs_ref),
        (wu_hbm, wu_ref), (wd_hbm, wd_ref),
    )
    loads = [
        pltpu.make_async_copy(src, dst, load_sem.at[i]) for i, (src, dst) in enumerate(sources)
    ]
    far = jnp.where(side == 0, 2, -2)
    near = jnp.where(core == 0, 1, -1)
    offsets = [jnp.int32(0), near, far, -far, -near]
    masks = [
        pltpu.make_async_copy(
            mask_hbm.at[0, offsets[i] + REACH], mask_ref.at[i], mask_sem.at[i]
        )
        for i in range(2 * REACH + 1)
    ]
    for i in range(5):
        loads[i].start()
    for mask_load in masks:
        mask_load.start()
    for i in range(5, len(loads)):
        loads[i].start()

    step_rows = rows // CHUNKS

    def chunk(c):
        return pl.ds(c * step_rows, step_rows)

    def copy(source, target, c, sem, device):
        return pltpu.make_async_remote_copy(
            src_ref=slab_ref.at[source, chunk(c)], dst_ref=slab_ref.at[target, chunk(c)],
            send_sem=sem.at[c], recv_sem=recv.at[target, c],
            device_id={"blk": device}, device_id_type=MESH,
        )

    def partner_copy(c):
        return copy(OWN, PARTNER, c, p_send, partner)

    def mirror_copy(c):
        return copy(OWN, MIRROR, c, m_send, mirror)

    def rail_copy(c):
        return copy(MIRROR, RAIL, c, r_send, rail_to)

    def cross_copy(c, source):
        return copy(source, CROSS, c, c_send, partner)

    def got_mirror(c):
        mirror_copy(c).wait_recv()
        rail_copy(c).start()

        @pl.when(same)
        def _():
            cross_copy(c, MIRROR).start()

    def got_rail(c):
        rail_copy(c).wait_recv()

        @pl.when(jnp.logical_not(same))
        def _():
            cross_copy(c, RAIL).start()

    def got_cross(c, when):
        @pl.when(when)
        def _():
            cross_copy(c, RAIL).wait_recv()

    loads[0].wait()
    pl.semaphore_wait(barrier, n - 1)
    for c in range(CHUNKS):
        mirror_copy(c).start()
    for c in range(CHUNKS):
        partner_copy(c).start()

    def normalize(value):
        full = value.astype(jnp.float32)
        return (
            full * lax.rsqrt(jnp.mean(full * full, axis=-1, keepdims=True) + 1e-06) * ng_ref[...]
        ).astype(jnp.bfloat16)

    def set_bias(i):
        @pl.when(i == 0)
        def _():
            masks[0].wait()

        for j in range(1, 2 * REACH + 1):
            @pl.when(i == j)
            def _():
                masks[j].wait()

        for k in range(rows // PAIR):
            span = slice(k * PAIR, (k + 1) * PAIR)
            bias_ref[i, span, :] = jnp.where(mask_ref[i, :, span] > 0, 0.0, NEG).T

    def unit(slot, start, count):
        normed = normalize(slab_ref[slot, pl.ds(start, count), :])
        kb_ref[:count] = jnp.dot(
            normed, wk_ref[...], preferred_element_type=jnp.float32
        ).astype(jnp.bfloat16)
        values = lax.dot_general(
            wvt_ref[...], normed, (((1,), (1,)), ((), ())), preferred_element_type=jnp.float32
        ).astype(jnp.bfloat16)
        for h in range(heads):
            vt_ref[h, :HEAD_DIM, :count] = values[h * HEAD_DIM:(h + 1) * HEAD_DIM]

        def scores(h):
            pair = h // 2
            piece = kb_ref[:count, pair * PAIR:(pair + 1) * PAIR]
            return jnp.dot(
                jnp.concatenate([piece, piece], axis=1), qt_ref[h],
                preferred_element_type=jnp.float32,
            ) + bias_ref[slot, pl.ds(start, count), :]

        def finish(h, score):
            old = m_ref[h]
            new = jnp.maximum(old, jnp.max(score, axis=0, keepdims=True))
            m_ref[h] = new
            weight = jnp.exp2(score - new).astype(jnp.bfloat16)
            result = jnp.dot(vt_ref[h, :, :count], weight, preferred_element_type=jnp.float32)
            acc_ref[h] = acc_ref[h] * jnp.exp2(old - new) + result

        ahead = scores(0)
        for h in range(heads):
            current = ahead
            if h + 1 < heads:
                ahead = scores(h + 1)
            finish(h, current)

    ones = jnp.ones((heads, SUMS, vt_ref.shape[2]), jnp.bfloat16)
    vt_ref[:, HEAD_DIM:, :] = ones
    m_ref[...] = jnp.full(m_ref.shape, NEG, jnp.float32)
    acc_ref[...] = jnp.zeros(acc_ref.shape, jnp.float32)

    loads[1].wait()
    normed = normalize(slab_ref[OWN])
    loads[2].wait()
    wqt = wq_ref[...].T
    query = lax.dot_general(
        wqt, normed, (((1,), (1,)), ((), ())), preferred_element_type=jnp.float32
    ).astype(jnp.bfloat16).astype(jnp.float32) * SCALE
    high = query.astype(jnp.bfloat16)
    low = (query - high.astype(jnp.float32)).astype(jnp.bfloat16)
    zero = jnp.zeros((HEAD_DIM, rows), jnp.bfloat16)
    for h in range(heads):
        span = slice(h * HEAD_DIM, (h + 1) * HEAD_DIM)
        for part, base in ((high, 0), (low, PAIR)):
            here = base + (h % 2) * HEAD_DIM
            there = base + (1 - h % 2) * HEAD_DIM
            qt_ref[h, here:here + HEAD_DIM] = part[span]
            qt_ref[h, there:there + HEAD_DIM] = zero
    loads[4].wait()
    wvt_ref[...] = wv_ref[...].T
    loads[3].wait()
    set_bias(0)
    eye = lax.broadcasted_iota(jnp.int32, (rows, rows), 0) == lax.broadcasted_iota(
        jnp.int32, (rows, rows), 1
    )
    bias_ref[0] = jnp.where(eye, 0.0, bias_ref[0])

    per = CHUNKS // PARTS
    half = rows // 2
    quarter = rows // PARTS

    events = {
        0: (),
        1: (),
        2: (("p", 0, 8),),
        3: (("m", 0, 1),),
        4: (("m", 1, 4), ("r", 0, 1)),
        5: (
            ("m", 4, 5), ("r", 1, 2), ("m", 5, 6), ("r", 2, 3), ("m", 6, 7), ("r", 3, 4),
            ("x", 0, 4),
        ),
        6: (("m", 7, 8), ("r", 4, 5), ("y", 0, 4)),
        7: (("r", 5, 6),),
    }
    late_events = {
        0: (("r", 6, 7), ("x", 4, 6)),
        1: (("y", 4, 6),),
        2: (("r", 7, 8), ("x", 6, 8)),
        3: (("y", 6, 8),),
    }
    actions = {
        "p": lambda c: partner_copy(c).wait_recv(),
        "m": got_mirror, "r": got_rail,
        "x": lambda c: got_cross(c, jnp.logical_not(same)),
        "y": lambda c: got_cross(c, same),
    }

    def run_events(u, table):
        for k, listed in table.items():
            if listed:
                @pl.when(u == k)
                def _():
                    for kind, low_c, high_c in listed:
                        for c in range(low_c, high_c):
                            actions[kind](c)

    def step(u, carry):
        run_events(u, events)
        slot = jnp.where(
            u < 4, u // 2,
            jnp.where(u == 5, late_one, jnp.where(u == 6, late_two, MIRROR)),
        )
        start = jnp.where(u < 4, u % 2, jnp.where(u == 7, 1, 0)) * half
        unit(slot, start, half)

        @pl.when(u < 2 * REACH)
        def _():
            set_bias(u + 1)
        return carry

    lax.fori_loop(0, 8, step, 0)

    def late_step(v, carry):
        run_events(v, late_events)
        slot = jnp.where(v % 2 == 0, late_one, late_two)
        unit(slot, half + (v // 2) * quarter, quarter)
        return carry

    lax.fori_loop(0, 4, late_step, 0)

    for h in range(heads):
        total = acc_ref[h, HEAD_DIM:HEAD_DIM + 1]
        mixed_ref[h * HEAD_DIM:(h + 1) * HEAD_DIM, :] = (
            acc_ref[h, :HEAD_DIM] / total
        ).astype(jnp.bfloat16)
    for load in loads[5:]:
        load.wait()
    after_ref[...] = slab_ref[OWN].astype(jnp.float32) + jnp.dot(
        mixed_ref[...].T, wo_ref[...], preferred_element_type=jnp.float32
    )

    local_mean = jnp.sum(after_ref[...], axis=0, keepdims=True) * (1.0 / rows)
    spread = after_ref[...] - local_mean
    stats_ref[0, 0:1] = local_mean
    stats_ref[0, 1:2] = jnp.sum(spread * spread, axis=0, keepdims=True)

    def stats_copy(d):
        return pltpu.make_async_remote_copy(
            src_ref=stats_ref.at[0], dst_ref=stats_ref.at[d],
            send_sem=s_send.at[d], recv_sem=s_recv.at[d],
            device_id={"blk": lax.rem(me + d, n)}, device_id_type=MESH,
        )

    def send_stats(d, carry):
        stats_copy(d).start()
        return carry

    def take_stats(d, carry):
        stats_copy(d).wait_recv()
        return carry

    lax.fori_loop(1, n, send_stats, 0)

    for c in range(CHUNKS):
        partner_copy(c).wait_send()
        mirror_copy(c).wait_send()
        rail_copy(c).wait_send()
        cross_copy(c, RAIL).wait_send()

    lax.fori_loop(1, n, take_stats, 0)
    gathered = stats_ref[...]
    means = gathered[:, 0, :]
    mean = jnp.sum(means, axis=0, keepdims=True) * (1.0 / n)
    shifts = means - mean
    var = (
        jnp.sum(gathered[:, 1, :], axis=0, keepdims=True) * (1.0 / rows)
        + jnp.sum(shifts * shifts, axis=0, keepdims=True)
    ) * (1.0 / n)
    gain = lax.rsqrt(var + 1e-05) * bg_ref[...]
    batched = ((after_ref[...] - mean) * gain + bs_ref[...]).astype(jnp.bfloat16)
    hidden = jax.nn.gelu(
        jnp.dot(batched, wu_ref[...], preferred_element_type=jnp.float32), approximate=True
    ).astype(jnp.bfloat16)
    out_ref[...] = (
        after_ref[...] + jnp.dot(hidden, wd_ref[...], preferred_element_type=jnp.float32)
    ).astype(jnp.bfloat16)

    def sent_stats(d, carry):
        stats_copy(d).wait_send()
        return carry

    lax.fori_loop(1, n, sent_stats, 0)


def body(
    atoms, edge_mask, norm_gain, w_query, w_key, w_value, w_out, bn_gain, bn_shift, w_up, w_down
):
    n = lax.axis_size("blk")
    rows, width = atoms.shape
    ff = w_up.shape[1]
    slabs = edge_mask.shape[1]
    heads = width // HEAD_DIM
    half = rows // 2
    bf16, f32 = jnp.bfloat16, jnp.float32
    dma = pltpu.SemaphoreType.DMA
    return pl.pallas_call(
        functools.partial(kernel, n),
        out_shape=jax.ShapeDtypeStruct((rows, width), bf16),
        in_specs=[pl.BlockSpec(memory_space=pl.ANY)] * 11,
        out_specs=pl.BlockSpec(memory_space=pltpu.VMEM),
        scratch_shapes=[
            pltpu.VMEM((slabs, rows, width), bf16),
            pltpu.VMEM((slabs, rows, rows), jnp.int32),
            pltpu.VMEM((1, width), f32),
            pltpu.VMEM((width, width), bf16),
            pltpu.VMEM((width, width), bf16),
            pltpu.VMEM((width, width), bf16),
            pltpu.VMEM((width, width), bf16),
            pltpu.VMEM((1, width), f32),
            pltpu.VMEM((1, width), f32),
            pltpu.VMEM((width, ff), bf16),
            pltpu.VMEM((ff, width), bf16),
            pltpu.VMEM((width, width), bf16),
            pltpu.VMEM((heads, 2 * PAIR, rows), bf16),
            pltpu.VMEM((half, width), bf16),
            pltpu.VMEM((heads, HEAD_DIM + SUMS, half), bf16),
            pltpu.VMEM((slabs, rows, rows), f32),
            pltpu.VMEM((heads, 1, rows), f32),
            pltpu.VMEM((heads, HEAD_DIM + SUMS, rows), f32),
            pltpu.VMEM((width, rows), bf16),
            pltpu.VMEM((rows, width), f32),
            pltpu.VMEM((n, 2, width), f32),
            dma((10,)),
            dma((slabs,)),
            dma((CHUNKS,)), dma((CHUNKS,)), dma((CHUNKS,)), dma((CHUNKS,)),
            dma((slabs, CHUNKS)),
            dma((n,)), dma((n,)),
        ],
        compiler_params=pltpu.CompilerParams(
            collective_id=0, has_side_effects=True, vmem_limit_bytes=60 * 1024 * 1024
        ),
    )(
        atoms, edge_mask, norm_gain.reshape(1, width), w_query, w_key, w_value, w_out,
        bn_gain.reshape(1, width), bn_shift.reshape(1, width), w_up, w_down,
    )


def solution(mesh):
    placed = (
        P(("grp", "blk"), None),
        P(("grp", "blk"), None, None, None),
        P(), P(), P(), P(), P(), P(), P(), P(), P(),
    )
    return jax.shard_map(
        body, mesh=mesh, in_specs=placed, out_specs=P(("grp", "blk"), None), check_vma=False
    )
```

time: 42.7 us -> 49.1 us (1.15)
  Pallas kernels: 40.7 us -> 47.1 us
    pallas_call x1, Pallas kernels: 40.7 us -> 47.1 us  [body(): pl.pallas_call(functools.partial(kernel, n), out_shape=jax.ShapeDtypeStru...]
where the time goes in v1:
time: 49.1 us; the launch traced here: 48.9 us
  Pallas kernels  47.1 us (96%)
  local copies, waits for them, and re-layouts  1.87 us (4%)
    pallas_call x1, Pallas kernels, body(): pl.pallas_call(functools.partial(kernel, n), out_shape=jax.ShapeDtypeStru...  47.1 us
    unnamed x1, local copies, waits for them, and re-layouts  1.87 us

profile of v1, /device:TPU:0, one launch (start us, length us, event | category | flops | bytes accessed | tf_op | source)
XLA Modules:
  0.0 48.9 jit_solution(10051041820382872851)
XLA Ops:
  0.0 47.1 %shard_map.109 = bf16[512,512]{1,0:T(8,128)(2,1)} custom-call(bf16[512,512]{1,0:T(8,128)(2,1)} %atoms_hbm.1, s32[1,5,512,512]{3,2,1,0:T(8,128)} %mask_hbm.1, f32[1,512]{1,0:T(1,128)} %bitcast.3, bf16[512,512]{1,0:T(8,128)(2,1)} %wq_hbm.1, bf16[512,512]{1,0:T(8,128)(2,1)} %wk_hbm.1, bf16[512,512]{1,0:T(8,128)(2,1)} %wv_hbm.1, bf16[512,512]{1,0:T(8,128)(2,1)} %wo_hbm.1, ...), custom_call_target="tpu_custom_call" | custom-call | tf_op jit(solution)/shard_map/pallas_call | solution.py:353
  47.1 1.9 %copy.13 = bf16[512,512]{1,0:T(8,128)(2,1)} copy(bf16[512,512]{1,0:T(8,128)(2,1)} %shard_map.109) | data formatting | bytes 1048576

commit v2 on v1

--- a/solution.py
+++ b/solution.py
@@ -14,6 +14,8 @@
 CHUNKS = 8
 PARTS = 4
 SUMS = 16
+LOOK = 3
+SLOTS = LOOK + 1
 NEG = -1e30
 MESH = pl.DeviceIdType.MESH
 OWN, PARTNER, MIRROR, RAIL, CROSS = 0, 1, 2, 3, 4
@@ -25,15 +27,16 @@
     atoms_hbm, mask_hbm, ng_hbm, wq_hbm, wk_hbm, wv_hbm, wo_hbm, bg_hbm, bs_hbm, wu_hbm, wd_hbm,
     out_ref,
     slab_ref, mask_ref, ng_ref, wq_ref, wk_ref, wv_ref, wo_ref, bg_ref, bs_ref, wu_ref, wd_ref,
-    wvt_ref, qt_ref, kb_ref, vt_ref, bias_ref, m_ref, acc_ref, mixed_ref, after_ref,
+    wvt_ref, qt_ref, kb_ref, vt_ref, bias_ref, m_ref, s_ref, acc_ref, mixed_ref, after_ref,
     stats_ref, load_sem, mask_sem,
-    p_send, m_send, r_send, c_send, recv, s_send, s_recv,
+    p_send, m_send, r_send, c_send, recv, s_send, s_recv, up_sem, down_sem,
 ):
     me = lax.axis_index("blk")
     rows, width = after_ref.shape
     heads = width // HEAD_DIM
     group, inside = me // 4, me % 4
     side, core = inside // 2, inside % 2
+    cousin = group * 4 + (1 - side) * 2 + (1 - core)
     partner = group * 4 + side * 2 + (1 - core)
     mirror = group * 4 + (1 - side) * 2 + core
     groups = n // 4
@@ -44,17 +47,61 @@
 
     barrier = pltpu.get_barrier_semaphore()
 
-    def greet(d, carry):
-        pl.semaphore_signal(
-            barrier, inc=1, device_id={"blk": lax.rem(me + d, n)}, device_id_type=MESH
-        )
-        return carry
-
-    lax.fori_loop(1, n, greet, 0)
+    for known in (partner, mirror, cousin):
+        pl.semaphore_signal(barrier, inc=1, device_id={"blk": known}, device_id_type=MESH)
+
+    @pl.when(group > 0)
+    def _():
+        pl.semaphore_signal(barrier, inc=1, device_id={"blk": me - 4}, device_id_type=MESH)
+
+    @pl.when(group < groups - 1)
+    def _():
+        pl.semaphore_signal(barrier, inc=1, device_id={"blk": me + 4}, device_id_type=MESH)
+
+    def tell_up():
+        @pl.when(group < groups - 1)
+        def _():
+            pl.semaphore_signal(up_sem, inc=1, device_id={"blk": me + 4}, device_id_type=MESH)
+
+    def tell_down():
+        @pl.when(group > 0)
+        def _():
+            pl.semaphore_signal(down_sem, inc=1, device_id={"blk": me - 4}, device_id_type=MESH)
+
+    def roll_call_start():
+        @pl.when(group == 0)
+        def _():
+            tell_up()
+
+        @pl.when(group == groups - 1)
+        def _():
+            tell_down()
+
+    def roll_call_early():
+        @pl.when(group == 1)
+        def _():
+            pl.semaphore_wait(up_sem, 1)
+            tell_up()
+
+        @pl.when(group == groups - 2)
+        def _():
+            pl.semaphore_wait(down_sem, 1)
+            tell_down()
+
+    def roll_call_end():
+        @pl.when(group > 1)
+        def _():
+            pl.semaphore_wait(up_sem, 1)
+            tell_up()
+
+        @pl.when(group < groups - 2)
+        def _():
+            pl.semaphore_wait(down_sem, 1)
+            tell_down()
 
     sources = (
-        (atoms_hbm, slab_ref.at[OWN]), (ng_hbm, ng_ref), (wq_hbm, wq_ref), (wk_hbm, wk_ref),
-        (wv_hbm, wv_ref), (wo_hbm, wo_ref), (bg_hbm, bg_ref), (bs_hbm, bs_ref),
+        (atoms_hbm, slab_ref.at[OWN]), (ng_hbm, ng_ref.at[0:1]), (wq_hbm, wq_ref), (wk_hbm, wk_ref),
+        (wv_hbm, wv_ref), (wo_hbm, wo_ref), (bg_hbm, bg_ref.at[0:1]), (bs_hbm, bs_ref.at[0:1]),
         (wu_hbm, wu_ref), (wd_hbm, wd_ref),
     )
     loads = [
@@ -121,16 +168,19 @@
             cross_copy(c, RAIL).wait_recv()
 
     loads[0].wait()
-    pl.semaphore_wait(barrier, n - 1)
+    pl.semaphore_wait(
+        barrier, 3 + (group > 0).astype(jnp.int32) + (group < groups - 1).astype(jnp.int32)
+    )
     for c in range(CHUNKS):
         mirror_copy(c).start()
     for c in range(CHUNKS):
         partner_copy(c).start()
+    roll_call_start()
 
     def normalize(value):
         full = value.astype(jnp.float32)
         return (
-            full * lax.rsqrt(jnp.mean(full * full, axis=-1, keepdims=True) + 1e-06) * ng_ref[...]
+            full * lax.rsqrt(jnp.mean(full * full, axis=-1, keepdims=True) + 1e-06) * ng_ref[0:1]
         ).astype(jnp.bfloat16)
 
     def set_bias(i):
@@ -161,25 +211,26 @@
         def scores(h):
             pair = h // 2
             piece = kb_ref[:count, pair * PAIR:(pair + 1) * PAIR]
-            return jnp.dot(
+            score = jnp.dot(
                 jnp.concatenate([piece, piece], axis=1), qt_ref[h],
                 preferred_element_type=jnp.float32,
             ) + bias_ref[slot, pl.ds(start, count), :]
-
-        def finish(h, score):
-            old = m_ref[h]
-            new = jnp.maximum(old, jnp.max(score, axis=0, keepdims=True))
-            m_ref[h] = new
-            weight = jnp.exp2(score - new).astype(jnp.bfloat16)
+            s_ref[h % SLOTS, :count] = score
+            return jnp.max(score, axis=0, keepdims=True)
+
+        def finish(h, peak):
+            old = m_ref[h, 0:1]
+            new = jnp.maximum(old, peak)
+            m_ref[h, 0:1] = new
+            weight = jnp.exp2(s_ref[h % SLOTS, :count] - new).astype(jnp.bfloat16)
             result = jnp.dot(vt_ref[h, :, :count], weight, preferred_element_type=jnp.float32)
             acc_ref[h] = acc_ref[h] * jnp.exp2(old - new) + result
 
-        ahead = scores(0)
+        peaks = [scores(h) for h in range(LOOK)]
         for h in range(heads):
-            current = ahead
-            if h + 1 < heads:
-                ahead = scores(h + 1)
-            finish(h, current)
+            if h + LOOK < heads:
+                peaks.append(scores(h + LOOK))
+            finish(h, peaks[h])
 
     ones = jnp.ones((heads, SUMS, vt_ref.shape[2]), jnp.bfloat16)
     vt_ref[:, HEAD_DIM:, :] = ones
@@ -203,6 +254,7 @@
             there = base + (1 - h % 2) * HEAD_DIM
             qt_ref[h, here:here + HEAD_DIM] = part[span]
             qt_ref[h, there:there + HEAD_DIM] = zero
+    roll_call_early()
     loads[4].wait()
     wvt_ref[...] = wv_ref[...].T
     loads[3].wait()
@@ -212,7 +264,13 @@
     )
     bias_ref[0] = jnp.where(eye, 0.0, bias_ref[0])
 
-    per = CHUNKS // PARTS
+    def more_bias(i, carry):
+        set_bias(i)
+        return carry
+
+    lax.fori_loop(1, 2 * REACH + 1, more_bias, 0)
+
+    roll_call_end()
     half = rows // 2
     quarter = rows // PARTS
 
@@ -259,10 +317,6 @@
         )
         start = jnp.where(u < 4, u % 2, jnp.where(u == 7, 1, 0)) * half
         unit(slot, start, half)
-
-        @pl.when(u < 2 * REACH)
-        def _():
-            set_bias(u + 1)
         return carry
 
     lax.fori_loop(0, 8, step, 0)
@@ -323,8 +377,8 @@
         jnp.sum(gathered[:, 1, :], axis=0, keepdims=True) * (1.0 / rows)
         + jnp.sum(shifts * shifts, axis=0, keepdims=True)
     ) * (1.0 / n)
-    gain = lax.rsqrt(var + 1e-05) * bg_ref[...]
-    batched = ((after_ref[...] - mean) * gain + bs_ref[...]).astype(jnp.bfloat16)
+    gain = lax.rsqrt(var + 1e-05) * bg_ref[0:1]
+    batched = ((after_ref[...] - mean) * gain + bs_ref[0:1]).astype(jnp.bfloat16)
     hidden = jax.nn.gelu(
         jnp.dot(batched, wu_ref[...], preferred_element_type=jnp.float32), approximate=True
     ).astype(jnp.bfloat16)
@@ -352,19 +406,19 @@
     dma = pltpu.SemaphoreType.DMA
     return pl.pallas_call(
         functools.partial(kernel, n),
-        out_shape=jax.ShapeDtypeStruct((rows, width), bf16),
+        out_shape=pltpu.VMEM((rows, width), bf16),
         in_specs=[pl.BlockSpec(memory_space=pl.ANY)] * 11,
         out_specs=pl.BlockSpec(memory_space=pltpu.VMEM),
         scratch_shapes=[
             pltpu.VMEM((slabs, rows, width), bf16),
             pltpu.VMEM((slabs, rows, rows), jnp.int32),
-            pltpu.VMEM((1, width), f32),
+            pltpu.VMEM((8, width), f32),
             pltpu.VMEM((width, width), bf16),
             pltpu.VMEM((width, width), bf16),
             pltpu.VMEM((width, width), bf16),
             pltpu.VMEM((width, width), bf16),
-            pltpu.VMEM((1, width), f32),
-            pltpu.VMEM((1, width), f32),
+            pltpu.VMEM((8, width), f32),
+            pltpu.VMEM((8, width), f32),
             pltpu.VMEM((width, ff), bf16),
             pltpu.VMEM((ff, width), bf16),
             pltpu.VMEM((width, width), bf16),
@@ -372,7 +426,8 @@
             pltpu.VMEM((half, width), bf16),
             pltpu.VMEM((heads, HEAD_DIM + SUMS, half), bf16),
             pltpu.VMEM((slabs, rows, rows), f32),
-            pltpu.VMEM((heads, 1, rows), f32),
+            pltpu.VMEM((heads, 8, rows), f32),
+            pltpu.VMEM((SLOTS, half, rows), f32),
             pltpu.VMEM((heads, HEAD_DIM + SUMS, rows), f32),
             pltpu.VMEM((width, rows), bf16),
             pltpu.VMEM((rows, width), f32),
@@ -382,6 +437,7 @@
             dma((CHUNKS,)), dma((CHUNKS,)), dma((CHUNKS,)), dma((CHUNKS,)),
             dma((slabs, CHUNKS)),
             dma((n,)), dma((n,)),
+            pltpu.SemaphoreType.REGULAR, pltpu.SemaphoreType.REGULAR,
         ],
         compiler_params=pltpu.CompilerParams(
             collective_id=0, has_side_effects=True, vmem_limit_bytes=60 * 1024 * 1024

time: 49.1 us -> 40.5 us (0.82)
  Pallas kernels: 47.1 us -> 39.5 us
  local copies, waits for them, and re-layouts: 1.87 us -> 0.8 us
    pallas_call x1, Pallas kernels: 47.1 us -> 39.5 us  [body(): pl.pallas_call(functools.partial(kernel, n), out_shape=pltpu.VMEM((rows,...]
    unnamed x1, local copies, waits for them, and re-layouts: 1.87 us -> 0.8 us
where the time goes in v2:
time: 40.5 us; the launch traced here: 40.3 us
  Pallas kernels  39.5 us (98%)
  local copies, waits for them, and re-layouts  0.8 us (2%)
    pallas_call x1, Pallas kernels, body(): pl.pallas_call(functools.partial(kernel, n), out_shape=pltpu.VMEM((rows,...  39.5 us

profile of v2, /device:TPU:0, one launch (start us, length us, event | category | flops | bytes accessed | tf_op | source)
XLA Modules:
  0.0 40.3 jit_solution(17994293849480305)
XLA Ops:
  0.0 39.5 %shard_map.109 = bf16[512,512]{1,0:T(8,128)(2,1)S(1)} custom-call(bf16[512,512]{1,0:T(8,128)(2,1)} %atoms_hbm.1, s32[1,5,512,512]{3,2,1,0:T(8,128)} %mask_hbm.1, f32[1,512]{1,0:T(1,128)} %bitcast.3, bf16[512,512]{1,0:T(8,128)(2,1)} %wq_hbm.1, bf16[512,512]{1,0:T(8,128)(2,1)} %wk_hbm.1, bf16[512,512]{1,0:T(8,128)(2,1)} %wv_hbm.1, bf16[512,512]{1,0:T(8,128)(2,1)} %wo_hbm.1, ...), custom_call_target="tpu_custom_call" | custom-call | tf_op jit(solution)/shard_map/pallas_call | solution.py:407
  39.5 0.8 %copy.13 = bf16[512,512]{1,0:T(8,128)(2,1)} copy(bf16[512,512]{1,0:T(8,128)(2,1)S(1)} %shard_map.109) | data formatting | bytes 1048576

commit v3 on v2

--- a/solution.py
+++ b/solution.py
@@ -12,7 +12,6 @@
 PAIR = 2 * HEAD_DIM
 REACH = 2
 CHUNKS = 8
-PARTS = 4
 SUMS = 16
 LOOK = 3
 SLOTS = LOOK + 1
@@ -27,7 +26,7 @@
     atoms_hbm, mask_hbm, ng_hbm, wq_hbm, wk_hbm, wv_hbm, wo_hbm, bg_hbm, bs_hbm, wu_hbm, wd_hbm,
     out_ref,
     slab_ref, mask_ref, ng_ref, wq_ref, wk_ref, wv_ref, wo_ref, bg_ref, bs_ref, wu_ref, wd_ref,
-    wvt_ref, qt_ref, kb_ref, vt_ref, bias_ref, m_ref, s_ref, acc_ref, mixed_ref, after_ref,
+    wvt_ref, qt_ref, normed_ref, kb_ref, vt_ref, bias_ref, m_ref, s_ref, acc_ref, mixed_ref, after_ref,
     stats_ref, load_sem, mask_sem,
     p_send, m_send, r_send, c_send, recv, s_send, s_recv, up_sem, down_sem,
 ):
@@ -183,47 +182,46 @@
             full * lax.rsqrt(jnp.mean(full * full, axis=-1, keepdims=True) + 1e-06) * ng_ref[0:1]
         ).astype(jnp.bfloat16)
 
-    def set_bias(i):
-        @pl.when(i == 0)
-        def _():
-            masks[0].wait()
-
-        for j in range(1, 2 * REACH + 1):
-            @pl.when(i == j)
-            def _():
-                masks[j].wait()
-
-        for k in range(rows // PAIR):
-            span = slice(k * PAIR, (k + 1) * PAIR)
-            bias_ref[i, span, :] = jnp.where(mask_ref[i, :, span] > 0, 0.0, NEG).T
-
-    def unit(slot, start, count):
-        normed = normalize(slab_ref[slot, pl.ds(start, count), :])
-        kb_ref[:count] = jnp.dot(
-            normed, wk_ref[...], preferred_element_type=jnp.float32
+    def unit(pieces, count):
+        total = len(pieces) * count
+        for i, (slot, start) in enumerate(pieces):
+            normed_ref[i * count:(i + 1) * count] = normalize(
+                slab_ref[slot, pl.ds(start, count), :]
+            )
+        kb_ref[...] = jnp.dot(
+            normed_ref[...], wk_ref[...], preferred_element_type=jnp.float32
         ).astype(jnp.bfloat16)
         values = lax.dot_general(
-            wvt_ref[...], normed, (((1,), (1,)), ((), ())), preferred_element_type=jnp.float32
+            wvt_ref[...], normed_ref[...], (((1,), (1,)), ((), ())),
+            preferred_element_type=jnp.float32,
         ).astype(jnp.bfloat16)
         for h in range(heads):
-            vt_ref[h, :HEAD_DIM, :count] = values[h * HEAD_DIM:(h + 1) * HEAD_DIM]
+            vt_ref[h, :HEAD_DIM] = values[h * HEAD_DIM:(h + 1) * HEAD_DIM]
+        atom = lax.broadcasted_iota(jnp.int32, (rows, PAIR), 0)
+        other = lax.broadcasted_iota(jnp.int32, (rows, PAIR), 1)
+        for i, (slot, start) in enumerate(pieces):
+            linked = mask_ref[slot, :, pl.ds(pl.multiple_of(start, PAIR), PAIR)] > 0
+            shift = start + jnp.where(slot == OWN, 0, rows)
+            bias_ref[i * count:(i + 1) * count, :] = jnp.where(
+                linked | (atom == other + shift), 0.0, NEG
+            ).T
 
         def scores(h):
             pair = h // 2
-            piece = kb_ref[:count, pair * PAIR:(pair + 1) * PAIR]
+            piece = kb_ref[:total, pair * PAIR:(pair + 1) * PAIR]
             score = jnp.dot(
                 jnp.concatenate([piece, piece], axis=1), qt_ref[h],
                 preferred_element_type=jnp.float32,
-            ) + bias_ref[slot, pl.ds(start, count), :]
-            s_ref[h % SLOTS, :count] = score
+            ) + bias_ref[:total]
+            s_ref[h % SLOTS, :total] = score
             return jnp.max(score, axis=0, keepdims=True)
 
         def finish(h, peak):
             old = m_ref[h, 0:1]
             new = jnp.maximum(old, peak)
             m_ref[h, 0:1] = new
-            weight = jnp.exp2(s_ref[h % SLOTS, :count] - new).astype(jnp.bfloat16)
-            result = jnp.dot(vt_ref[h, :, :count], weight, preferred_element_type=jnp.float32)
+            weight = jnp.exp2(s_ref[h % SLOTS, :total] - new).astype(jnp.bfloat16)
+            result = jnp.dot(vt_ref[h, :, :total], weight, preferred_element_type=jnp.float32)
             acc_ref[h] = acc_ref[h] * jnp.exp2(old - new) + result
 
         peaks = [scores(h) for h in range(LOOK)]
@@ -258,76 +256,63 @@
     loads[4].wait()
     wvt_ref[...] = wv_ref[...].T
     loads[3].wait()
-    set_bias(0)
-    eye = lax.broadcasted_iota(jnp.int32, (rows, rows), 0) == lax.broadcasted_iota(
-        jnp.int32, (rows, rows), 1
-    )
-    bias_ref[0] = jnp.where(eye, 0.0, bias_ref[0])
-
-    def more_bias(i, carry):
-        set_bias(i)
-        return carry
-
-    lax.fori_loop(1, 2 * REACH + 1, more_bias, 0)
-
-    roll_call_end()
-    half = rows // 2
-    quarter = rows // PARTS
-
-    events = {
-        0: (),
-        1: (),
-        2: (("p", 0, 8),),
-        3: (("m", 0, 1),),
-        4: (("m", 1, 4), ("r", 0, 1)),
-        5: (
-            ("m", 4, 5), ("r", 1, 2), ("m", 5, 6), ("r", 2, 3), ("m", 6, 7), ("r", 3, 4),
-            ("x", 0, 4),
-        ),
-        6: (("m", 7, 8), ("r", 4, 5), ("y", 0, 4)),
-        7: (("r", 5, 6),),
-    }
-    late_events = {
-        0: (("r", 6, 7), ("x", 4, 6)),
-        1: (("y", 4, 6),),
-        2: (("r", 7, 8), ("x", 6, 8)),
-        3: (("y", 6, 8),),
-    }
+
     actions = {
         "p": lambda c: partner_copy(c).wait_recv(),
+        "e": lambda c: roll_call_end(),
         "m": got_mirror, "r": got_rail,
         "x": lambda c: got_cross(c, jnp.logical_not(same)),
         "y": lambda c: got_cross(c, same),
     }
 
+    def run(listed):
+        for kind, low_c, high_c in listed:
+            for c in range(low_c, high_c):
+                actions[kind](c)
+
     def run_events(u, table):
         for k, listed in table.items():
-            if listed:
-                @pl.when(u == k)
-                def _():
-                    for kind, low_c, high_c in listed:
-                        for c in range(low_c, high_c):
-                            actions[kind](c)
+            @pl.when(u == k)
+            def _():
+                run(listed)
+
+    half = rows // 2
 
     def step(u, carry):
-        run_events(u, events)
+        run_events(u, {
+            1: (("e", 0, 1), ("m", 0, 1)),
+            2: (("p", 0, 8), ("m", 1, 2)),
+            3: (("m", 2, 3),),
+            4: (("m", 3, 4),),
+            5: (
+                ("m", 4, 5), ("r", 0, 1), ("m", 5, 6), ("r", 1, 3), ("m", 6, 7), ("r", 3, 4),
+                ("x", 0, 4),
+            ),
+            6: (("m", 7, 8), ("r", 4, 5), ("y", 0, 4)),
+            7: (("r", 5, 6),),
+            8: (("r", 6, 7), ("x", 4, 6), ("y", 4, 6)),
+            9: (("r", 7, 8), ("x", 6, 8), ("y", 6, 8)),
+        })
+        for k, listed in ((0, (0,)), (2, (1,)), (4, (2,)), (5, (3, 4))):
+            @pl.when(u == k)
+            def _():
+                for i in listed:
+                    masks[i].wait()
         slot = jnp.where(
             u < 4, u // 2,
-            jnp.where(u == 5, late_one, jnp.where(u == 6, late_two, MIRROR)),
+            jnp.where((u == 4) | (u == 7), MIRROR, jnp.where(u == 6, late_two, late_one)),
         )
-        start = jnp.where(u < 4, u % 2, jnp.where(u == 7, 1, 0)) * half
-        unit(slot, start, half)
+        start = jnp.where(
+            u < 4, (u % 2) * half,
+            jnp.where(u < 7, 0, half + jnp.where(u == 9, PAIR, 0)),
+        )
+        slot_too = jnp.where(u < 8, slot, late_two)
+        start_too = jnp.where(u < 8, start + PAIR, start)
+        unit([(slot, start), (slot_too, start_too)], PAIR)
         return carry
 
-    lax.fori_loop(0, 8, step, 0)
-
-    def late_step(v, carry):
-        run_events(v, late_events)
-        slot = jnp.where(v % 2 == 0, late_one, late_two)
-        unit(slot, half + (v // 2) * quarter, quarter)
-        return carry
-
-    lax.fori_loop(0, 4, late_step, 0)
+    lax.fori_loop(0, 5, step, 0)
+    lax.fori_loop(5, 10, step, 0)
 
     for h in range(heads):
         total = acc_ref[h, HEAD_DIM:HEAD_DIM + 1]
@@ -401,7 +386,6 @@
     ff = w_up.shape[1]
     slabs = edge_mask.shape[1]
     heads = width // HEAD_DIM
-    half = rows // 2
     bf16, f32 = jnp.bfloat16, jnp.float32
     dma = pltpu.SemaphoreType.DMA
     return pl.pallas_call(
@@ -423,11 +407,12 @@
             pltpu.VMEM((ff, width), bf16),
             pltpu.VMEM((width, width), bf16),
             pltpu.VMEM((heads, 2 * PAIR, rows), bf16),
-            pltpu.VMEM((half, width), bf16),
-            pltpu.VMEM((heads, HEAD_DIM + SUMS, half), bf16),
-            pltpu.VMEM((slabs, rows, rows), f32),
+            pltpu.VMEM((2 * PAIR, width), bf16),
+            pltpu.VMEM((2 * PAIR, width), bf16),
+            pltpu.VMEM((heads, HEAD_DIM + SUMS, 2 * PAIR), bf16),
+            pltpu.VMEM((2 * PAIR, rows), f32),
             pltpu.VMEM((heads, 8, rows), f32),
-            pltpu.VMEM((SLOTS, half, rows), f32),
+            pltpu.VMEM((SLOTS, 2 * PAIR, rows), f32),
             pltpu.VMEM((heads, HEAD_DIM + SUMS, rows), f32),
             pltpu.VMEM((width, rows), bf16),
             pltpu.VMEM((rows, width), f32),

time: 40.5 us -> 35.3 us (0.87)
  Pallas kernels: 39.5 us -> 34.3 us
    pallas_call x1, Pallas kernels: 39.5 us -> 34.3 us  [body(): pl.pallas_call(functools.partial(kernel, n), out_shape=pltpu.VMEM((rows,...]
where the time goes in v3:
time: 35.3 us; the launch traced here: 35.1 us
  Pallas kernels  34.3 us (97%)
  local copies, waits for them, and re-layouts  0.8 us (2%)
    pallas_call x1, Pallas kernels, body(): pl.pallas_call(functools.partial(kernel, n), out_shape=pltpu.VMEM((rows,...  34.3 us
    unnamed x1, local copies, waits for them, and re-layouts  0.8 us

profile of v3, /device:TPU:0, one launch (start us, length us, event | category | flops | bytes accessed | tf_op | source)
XLA Modules:
  0.0 35.1 jit_solution(3070804206290951222)
XLA Ops:
  0.0 34.3 %shard_map.109 = bf16[512,512]{1,0:T(8,128)(2,1)S(1)} custom-call(bf16[512,512]{1,0:T(8,128)(2,1)} %atoms_hbm.1, s32[1,5,512,512]{3,2,1,0:T(8,128)} %mask_hbm.1, f32[1,512]{1,0:T(1,128)} %bitcast.3, bf16[512,512]{1,0:T(8,128)(2,1)} %wq_hbm.1, bf16[512,512]{1,0:T(8,128)(2,1)} %wk_hbm.1, bf16[512,512]{1,0:T(8,128)(2,1)} %wv_hbm.1, bf16[512,512]{1,0:T(8,128)(2,1)} %wo_hbm.1, ...), custom_call_target="tpu_custom_call" | custom-call | tf_op jit(solution)/shard_map/pallas_call | solution.py:391
  34.3 0.8 %copy.13 = bf16[512,512]{1,0:T(8,128)(2,1)} copy(bf16[512,512]{1,0:T(8,128)(2,1)S(1)} %shard_map.109) | data formatting | bytes 1048576

commit v4 on v3

--- a/solution.py
+++ b/solution.py
@@ -28,7 +28,7 @@
     slab_ref, mask_ref, ng_ref, wq_ref, wk_ref, wv_ref, wo_ref, bg_ref, bs_ref, wu_ref, wd_ref,
     wvt_ref, qt_ref, normed_ref, kb_ref, vt_ref, bias_ref, m_ref, s_ref, acc_ref, mixed_ref, after_ref,
     stats_ref, load_sem, mask_sem,
-    p_send, m_send, r_send, c_send, recv, s_send, s_recv, up_sem, down_sem,
+    p_send, p_recv, m_send, r_send, c_send, recv, s_send, s_recv, up_sem, down_sem,
 ):
     me = lax.axis_index("blk")
     rows, width = after_ref.shape
@@ -41,8 +41,6 @@
     groups = n // 4
     rail_to = ((group + 1 - 2 * side + groups) % groups) * 4 + side * 2 + core
     same = side == core
-    late_one = jnp.where(same, RAIL, CROSS)
-    late_two = jnp.where(same, CROSS, RAIL)
 
     barrier = pltpu.get_barrier_semaphore()
 
@@ -127,24 +125,31 @@
     def chunk(c):
         return pl.ds(c * step_rows, step_rows)
 
-    def copy(source, target, c, sem, device):
+    def copy(source, target, span, send, receive, device):
         return pltpu.make_async_remote_copy(
-            src_ref=slab_ref.at[source, chunk(c)], dst_ref=slab_ref.at[target, chunk(c)],
-            send_sem=sem.at[c], recv_sem=recv.at[target, c],
+            src_ref=slab_ref.at[source, span], dst_ref=slab_ref.at[target, span],
+            send_sem=send, recv_sem=receive,
             device_id={"blk": device}, device_id_type=MESH,
         )
 
-    def partner_copy(c):
-        return copy(OWN, PARTNER, c, p_send, partner)
+    def partner_copy():
+        return copy(OWN, PARTNER, pl.ds(0, rows), p_send, p_recv, partner)
 
     def mirror_copy(c):
-        return copy(OWN, MIRROR, c, m_send, mirror)
+        return copy(OWN, MIRROR, chunk(c), m_send, recv.at[0, c], mirror)
 
     def rail_copy(c):
-        return copy(MIRROR, RAIL, c, r_send, rail_to)
+        return copy(MIRROR, RAIL, chunk(c), r_send, recv.at[1, c], rail_to)
 
     def cross_copy(c, source):
-        return copy(source, CROSS, c, c_send, partner)
+        return copy(source, CROSS, chunk(c), c_send, recv.at[2, c], partner)
+
+    def sent():
+        for source, target, send, device in (
+            (OWN, PARTNER, p_send, partner), (OWN, MIRROR, m_send, mirror),
+            (MIRROR, RAIL, r_send, rail_to), (RAIL, CROSS, c_send, partner),
+        ):
+            copy(source, target, pl.ds(0, rows), send, p_recv, device).wait_send()
 
     def got_mirror(c):
         mirror_copy(c).wait_recv()
@@ -161,10 +166,8 @@
         def _():
             cross_copy(c, RAIL).start()
 
-    def got_cross(c, when):
-        @pl.when(when)
-        def _():
-            cross_copy(c, RAIL).wait_recv()
+    def got_cross(c):
+        cross_copy(c, RAIL).wait_recv()
 
     loads[0].wait()
     pl.semaphore_wait(
@@ -172,8 +175,7 @@
     )
     for c in range(CHUNKS):
         mirror_copy(c).start()
-    for c in range(CHUNKS):
-        partner_copy(c).start()
+    partner_copy().start()
     roll_call_start()
 
     def normalize(value):
@@ -258,11 +260,10 @@
     loads[3].wait()
 
     actions = {
-        "p": lambda c: partner_copy(c).wait_recv(),
+        "p": lambda c: partner_copy().wait_recv(),
         "e": lambda c: roll_call_end(),
         "m": got_mirror, "r": got_rail,
-        "x": lambda c: got_cross(c, jnp.logical_not(same)),
-        "y": lambda c: got_cross(c, same),
+        "c": got_cross,
     }
 
     def run(listed):
@@ -281,33 +282,31 @@
     def step(u, carry):
         run_events(u, {
             1: (("e", 0, 1), ("m", 0, 1)),
-            2: (("p", 0, 8), ("m", 1, 2)),
+            2: (("p", 0, 1), ("m", 1, 2)),
             3: (("m", 2, 3),),
-            4: (("m", 3, 4),),
-            5: (
-                ("m", 4, 5), ("r", 0, 1), ("m", 5, 6), ("r", 1, 3), ("m", 6, 7), ("r", 3, 4),
-                ("x", 0, 4),
-            ),
-            6: (("m", 7, 8), ("r", 4, 5), ("y", 0, 4)),
-            7: (("r", 5, 6),),
-            8: (("r", 6, 7), ("x", 4, 6), ("y", 4, 6)),
-            9: (("r", 7, 8), ("x", 6, 8), ("y", 6, 8)),
+            4: (("m", 3, 5),),
+            5: (("r", 0, 1), ("m", 5, 6), ("r", 1, 2), ("c", 0, 2), ("r", 2, 3), ("m", 6, 7)),
+            6: (("r", 3, 4), ("m", 7, 8)),
+            7: (("r", 4, 5), ("c", 2, 4)),
+            8: (("r", 5, 6), ("c", 4, 6)),
+            9: (("r", 6, 8), ("c", 6, 8)),
         })
         for k, listed in ((0, (0,)), (2, (1,)), (4, (2,)), (5, (3, 4))):
             @pl.when(u == k)
             def _():
                 for i in listed:
                     masks[i].wait()
-        slot = jnp.where(
-            u < 4, u // 2,
-            jnp.where((u == 4) | (u == 7), MIRROR, jnp.where(u == 6, late_two, late_one)),
-        )
+        plain = (u < 5) | (u == 6)
+        slot = jnp.where(u < 4, u // 2, jnp.where(plain, MIRROR, RAIL))
         start = jnp.where(
             u < 4, (u % 2) * half,
-            jnp.where(u < 7, 0, half + jnp.where(u == 9, PAIR, 0)),
+            jnp.where(
+                plain, (u // 6) * half,
+                jnp.where(u == 5, 0, (u - 6) * PAIR),
+            ),
         )
-        slot_too = jnp.where(u < 8, slot, late_two)
-        start_too = jnp.where(u < 8, start + PAIR, start)
+        slot_too = jnp.where(plain, slot, CROSS)
+        start_too = jnp.where(plain, start + PAIR, start)
         unit([(slot, start), (slot_too, start_too)], PAIR)
         return carry
 
@@ -315,9 +314,9 @@
     lax.fori_loop(5, 10, step, 0)
 
     for h in range(heads):
-        total = acc_ref[h, HEAD_DIM:HEAD_DIM + 1]
+        inverse = 1.0 / acc_ref[h, HEAD_DIM:HEAD_DIM + 1]
         mixed_ref[h * HEAD_DIM:(h + 1) * HEAD_DIM, :] = (
-            acc_ref[h, :HEAD_DIM] / total
+            acc_ref[h, :HEAD_DIM] * inverse
         ).astype(jnp.bfloat16)
     for load in loads[5:]:
         load.wait()
@@ -330,30 +329,21 @@
     stats_ref[0, 0:1] = local_mean
     stats_ref[0, 1:2] = jnp.sum(spread * spread, axis=0, keepdims=True)
 
-    def stats_copy(d):
+    def stats_copy(source, target, device):
         return pltpu.make_async_remote_copy(
-            src_ref=stats_ref.at[0], dst_ref=stats_ref.at[d],
-            send_sem=s_send.at[d], recv_sem=s_recv.at[d],
-            device_id={"blk": lax.rem(me + d, n)}, device_id_type=MESH,
+            src_ref=stats_ref.at[source], dst_ref=stats_ref.at[target],
+            send_sem=s_send, recv_sem=s_recv,
+            device_id={"blk": device}, device_id_type=MESH,
         )
 
     def send_stats(d, carry):
-        stats_copy(d).start()
+        stats_copy(0, d, lax.rem(me + d, n)).start()
         return carry
 
-    def take_stats(d, carry):
-        stats_copy(d).wait_recv()
-        return carry
-
     lax.fori_loop(1, n, send_stats, 0)
-
-    for c in range(CHUNKS):
-        partner_copy(c).wait_send()
-        mirror_copy(c).wait_send()
-        rail_copy(c).wait_send()
-        cross_copy(c, RAIL).wait_send()
-
-    lax.fori_loop(1, n, take_stats, 0)
+    sent()
+    others = pl.ds(1, n - 1)
+    stats_copy(others, others, partner).wait_recv()
     gathered = stats_ref[...]
     means = gathered[:, 0, :]
     mean = jnp.sum(means, axis=0, keepdims=True) * (1.0 / n)
@@ -371,11 +361,7 @@
         after_ref[...] + jnp.dot(hidden, wd_ref[...], preferred_element_type=jnp.float32)
     ).astype(jnp.bfloat16)
 
-    def sent_stats(d, carry):
-        stats_copy(d).wait_send()
-        return carry
-
-    lax.fori_loop(1, n, sent_stats, 0)
+    stats_copy(others, others, partner).wait_send()
 
 
 def body(
@@ -419,9 +405,9 @@
             pltpu.VMEM((n, 2, width), f32),
             dma((10,)),
             dma((slabs,)),
-            dma((CHUNKS,)), dma((CHUNKS,)), dma((CHUNKS,)), dma((CHUNKS,)),
-            dma((slabs, CHUNKS)),
-            dma((n,)), dma((n,)),
+            dma, dma, dma, dma, dma,
+            dma((3, CHUNKS)),
+            dma, dma,
             pltpu.SemaphoreType.REGULAR, pltpu.SemaphoreType.REGULAR,
         ],
         compiler_params=pltpu.CompilerParams(

time: 35.3 us -> 33.9 us (0.960)
  Pallas kernels: 34.3 us -> 33 us
    pallas_call x1, Pallas kernels: 34.3 us -> 33 us  [body(): pl.pallas_call(functools.partial(kernel, n), out_shape=pltpu.VMEM((rows,...]
where the time goes in v4:
time: 33.9 us; the launch traced here: 33.8 us
  Pallas kernels  33 us (97%)
  local copies, waits for them, and re-layouts  0.8 us (2%)
    pallas_call x1, Pallas kernels, body(): pl.pallas_call(functools.partial(kernel, n), out_shape=pltpu.VMEM((rows,...  33 us
    unnamed x1, local copies, waits for them, and re-layouts  0.8 us

profile of v4, /device:TPU:0, one launch (start us, length us, event | category | flops | bytes accessed | tf_op | source)
XLA Modules:
  0.0 33.8 jit_solution(1305921441843621803)
XLA Ops:
  0.0 33.0 %shard_map.109 = bf16[512,512]{1,0:T(8,128)(2,1)S(1)} custom-call(bf16[512,512]{1,0:T(8,128)(2,1)} %atoms_hbm.1, s32[1,5,512,512]{3,2,1,0:T(8,128)} %mask_hbm.1, f32[1,512]{1,0:T(1,128)} %bitcast.3, bf16[512,512]{1,0:T(8,128)(2,1)} %wq_hbm.1, bf16[512,512]{1,0:T(8,128)(2,1)} %wk_hbm.1, bf16[512,512]{1,0:T(8,128)(2,1)} %wv_hbm.1, bf16[512,512]{1,0:T(8,128)(2,1)} %wo_hbm.1, ...), custom_call_target="tpu_custom_call" | custom-call | tf_op jit(solution)/shard_map/pallas_call | solution.py:377
  33.0 0.8 %copy.13 = bf16[512,512]{1,0:T(8,128)(2,1)} copy(bf16[512,512]{1,0:T(8,128)(2,1)S(1)} %shard_map.109) | data formatting | bytes 1048576

commit v5 on v4

--- a/solution.py
+++ b/solution.py
@@ -25,8 +25,8 @@
     n,
     atoms_hbm, mask_hbm, ng_hbm, wq_hbm, wk_hbm, wv_hbm, wo_hbm, bg_hbm, bs_hbm, wu_hbm, wd_hbm,
     out_ref,
-    slab_ref, mask_ref, ng_ref, wq_ref, wk_ref, wv_ref, wo_ref, bg_ref, bs_ref, wu_ref, wd_ref,
-    wvt_ref, qt_ref, normed_ref, kb_ref, vt_ref, bias_ref, m_ref, s_ref, acc_ref, mixed_ref, after_ref,
+    x_ref, slab_ref, mask_ref, ng_ref, wq_ref, wk_ref, wv_ref, wo_ref, bg_ref, bs_ref, wu_ref, wd_ref,
+    wvt_ref, qt_ref, kb_ref, vt_ref, bias_ref, m_ref, s_ref, acc_ref, mixed_ref, after_ref,
     stats_ref, load_sem, mask_sem,
     p_send, p_recv, m_send, r_send, c_send, recv, s_send, s_recv, up_sem, down_sem,
 ):
@@ -97,7 +97,7 @@
             tell_down()
 
     sources = (
-        (atoms_hbm, slab_ref.at[OWN]), (ng_hbm, ng_ref.at[0:1]), (wq_hbm, wq_ref), (wk_hbm, wk_ref),
+        (atoms_hbm, x_ref), (ng_hbm, ng_ref.at[0:1]), (wq_hbm, wq_ref), (wk_hbm, wk_ref),
         (wv_hbm, wv_ref), (wo_hbm, wo_ref), (bg_hbm, bg_ref.at[0:1]), (bs_hbm, bs_ref.at[0:1]),
         (wu_hbm, wu_ref), (wd_hbm, wd_ref),
     )
@@ -169,32 +169,33 @@
     def got_cross(c):
         cross_copy(c, RAIL).wait_recv()
 
-    loads[0].wait()
-    pl.semaphore_wait(
-        barrier, 3 + (group > 0).astype(jnp.int32) + (group < groups - 1).astype(jnp.int32)
-    )
-    for c in range(CHUNKS):
-        mirror_copy(c).start()
-    partner_copy().start()
-    roll_call_start()
-
     def normalize(value):
         full = value.astype(jnp.float32)
         return (
             full * lax.rsqrt(jnp.mean(full * full, axis=-1, keepdims=True) + 1e-06) * ng_ref[0:1]
         ).astype(jnp.bfloat16)
 
+    loads[0].wait()
+    loads[1].wait()
+    slab_ref[OWN] = normalize(x_ref[...])
+    pl.semaphore_wait(
+        barrier, 3 + (group > 0).astype(jnp.int32) + (group < groups - 1).astype(jnp.int32)
+    )
+    for c in range(CHUNKS):
+        mirror_copy(c).start()
+    partner_copy().start()
+    roll_call_start()
+
     def unit(pieces, count):
         total = len(pieces) * count
-        for i, (slot, start) in enumerate(pieces):
-            normed_ref[i * count:(i + 1) * count] = normalize(
-                slab_ref[slot, pl.ds(start, count), :]
-            )
+        normed = jnp.concatenate(
+            [slab_ref[slot, pl.ds(start, count), :] for slot, start in pieces], axis=0
+        )
         kb_ref[...] = jnp.dot(
-            normed_ref[...], wk_ref[...], preferred_element_type=jnp.float32
+            normed, wk_ref[...], preferred_element_type=jnp.float32
         ).astype(jnp.bfloat16)
         values = lax.dot_general(
-            wvt_ref[...], normed_ref[...], (((1,), (1,)), ((), ())),
+            wvt_ref[...], normed, (((1,), (1,)), ((), ())),
             preferred_element_type=jnp.float32,
         ).astype(jnp.bfloat16)
         for h in range(heads):
@@ -237,8 +238,7 @@
     m_ref[...] = jnp.full(m_ref.shape, NEG, jnp.float32)
     acc_ref[...] = jnp.zeros(acc_ref.shape, jnp.float32)
 
-    loads[1].wait()
-    normed = normalize(slab_ref[OWN])
+    normed = slab_ref[OWN]
     loads[2].wait()
     wqt = wq_ref[...].T
     query = lax.dot_general(
@@ -283,25 +283,28 @@
         run_events(u, {
             1: (("e", 0, 1), ("m", 0, 1)),
             2: (("p", 0, 1), ("m", 1, 2)),
-            3: (("m", 2, 3),),
-            4: (("m", 3, 5),),
-            5: (("r", 0, 1), ("m", 5, 6), ("r", 1, 2), ("c", 0, 2), ("r", 2, 3), ("m", 6, 7)),
-            6: (("r", 3, 4), ("m", 7, 8)),
+            3: (("m", 2, 4),),
+            4: (("m", 4, 5),),
+            5: (("r", 0, 1), ("m", 5, 6), ("r", 1, 2), ("c", 0, 2)),
+            6: (("m", 6, 7), ("r", 2, 4), ("m", 7, 8)),
             7: (("r", 4, 5), ("c", 2, 4)),
             8: (("r", 5, 6), ("c", 4, 6)),
             9: (("r", 6, 8), ("c", 6, 8)),
         })
-        for k, listed in ((0, (0,)), (2, (1,)), (4, (2,)), (5, (3, 4))):
+        for k, listed in ((0, (0,)), (2, (1,)), (3, (2,)), (5, (3, 4))):
             @pl.when(u == k)
             def _():
                 for i in listed:
                     masks[i].wait()
         plain = (u < 5) | (u == 6)
-        slot = jnp.where(u < 4, u // 2, jnp.where(plain, MIRROR, RAIL))
+        slot = jnp.where(
+            u < 3, u // 2,
+            jnp.where(u == 4, PARTNER, jnp.where(plain, MIRROR, RAIL)),
+        )
         start = jnp.where(
-            u < 4, (u % 2) * half,
+            u < 3, (u % 2) * half,
             jnp.where(
-                plain, (u // 6) * half,
+                plain, jnp.where(u == 3, 0, half),
                 jnp.where(u == 5, 0, (u - 6) * PAIR),
             ),
         )
@@ -320,7 +323,7 @@
         ).astype(jnp.bfloat16)
     for load in loads[5:]:
         load.wait()
-    after_ref[...] = slab_ref[OWN].astype(jnp.float32) + jnp.dot(
+    after_ref[...] = x_ref[...].astype(jnp.float32) + jnp.dot(
         mixed_ref[...].T, wo_ref[...], preferred_element_type=jnp.float32
     )
 
@@ -380,6 +383,7 @@
         in_specs=[pl.BlockSpec(memory_space=pl.ANY)] * 11,
         out_specs=pl.BlockSpec(memory_space=pltpu.VMEM),
         scratch_shapes=[
+            pltpu.VMEM((rows, width), bf16),
             pltpu.VMEM((slabs, rows, width), bf16),
             pltpu.VMEM((slabs, rows, rows), jnp.int32),
             pltpu.VMEM((8, width), f32),
@@ -393,7 +397,6 @@
             pltpu.VMEM((ff, width), bf16),
             pltpu.VMEM((width, width), bf16),
             pltpu.VMEM((heads, 2 * PAIR, rows), bf16),
-            pltpu.VMEM((2 * PAIR, width), bf16),
             pltpu.VMEM((2 * PAIR, width), bf16),
             pltpu.VMEM((heads, HEAD_DIM + SUMS, 2 * PAIR), bf16),
             pltpu.VMEM((2 * PAIR, rows), f32),

time: 33.9 us -> 32.7 us (0.965)
  Pallas kernels: 33 us -> 31.8 us
    pallas_call x1, Pallas kernels: 33 us -> 31.8 us  [body(): pl.pallas_call(functools.partial(kernel, n), out_shape=pltpu.VMEM((rows,...]
where the time goes in v5:
time: 32.7 us; the launch traced here: 32.6 us
  Pallas kernels  31.8 us (97%)
  local copies, waits for them, and re-layouts  0.8 us (2%)
    pallas_call x1, Pallas kernels, body(): pl.pallas_call(functools.partial(kernel, n), out_shape=pltpu.VMEM((rows,...  31.8 us
    unnamed x1, local copies, waits for them, and re-layouts  0.8 us

profile of v5, /device:TPU:0, one launch (start us, length us, event | category | flops | bytes accessed | tf_op | source)
XLA Modules:
  0.0 32.6 jit_solution(7224357594217572295)
XLA Ops:
  0.0 31.8 %shard_map.109 = bf16[512,512]{1,0:T(8,128)(2,1)S(1)} custom-call(bf16[512,512]{1,0:T(8,128)(2,1)} %atoms_hbm.1, s32[1,5,512,512]{3,2,1,0:T(8,128)} %mask_hbm.1, f32[1,512]{1,0:T(1,128)} %bitcast.3, bf16[512,512]{1,0:T(8,128)(2,1)} %wq_hbm.1, bf16[512,512]{1,0:T(8,128)(2,1)} %wk_hbm.1, bf16[512,512]{1,0:T(8,128)(2,1)} %wv_hbm.1, bf16[512,512]{1,0:T(8,128)(2,1)} %wo_hbm.1, ...), custom_call_target="tpu_custom_call" | custom-call | tf_op jit(solution)/shard_map/pallas_call | solution.py:380
  31.8 0.8 %copy.13 = bf16[512,512]{1,0:T(8,128)(2,1)} copy(bf16[512,512]{1,0:T(8,128)(2,1)S(1)} %shard_map.109) | data formatting | bytes 1048576

commit v6 on v5

--- a/solution.py
+++ b/solution.py
@@ -340,7 +340,8 @@
         )
 
     def send_stats(d, carry):
-        stats_copy(0, d, lax.rem(me + d, n)).start()
+        e = jnp.where(2 * group < groups, n - d, d)
+        stats_copy(0, e, lax.rem(me + e, n)).start()
         return carry
 
     lax.fori_loop(1, n, send_stats, 0)
@@ -356,13 +357,14 @@
         + jnp.sum(shifts * shifts, axis=0, keepdims=True)
     ) * (1.0 / n)
     gain = lax.rsqrt(var + 1e-05) * bg_ref[0:1]
-    batched = ((after_ref[...] - mean) * gain + bs_ref[0:1]).astype(jnp.bfloat16)
-    hidden = jax.nn.gelu(
-        jnp.dot(batched, wu_ref[...], preferred_element_type=jnp.float32), approximate=True
-    ).astype(jnp.bfloat16)
-    out_ref[...] = (
-        after_ref[...] + jnp.dot(hidden, wd_ref[...], preferred_element_type=jnp.float32)
-    ).astype(jnp.bfloat16)
+    for piece in (slice(0, half), slice(half, rows)):
+        batched = ((after_ref[piece] - mean) * gain + bs_ref[0:1]).astype(jnp.bfloat16)
+        hidden = jax.nn.gelu(
+            jnp.dot(batched, wu_ref[...], preferred_element_type=jnp.float32), approximate=True
+        ).astype(jnp.bfloat16)
+        out_ref[piece] = (
+            after_ref[piece] + jnp.dot(hidden, wd_ref[...], preferred_element_type=jnp.float32)
+        ).astype(jnp.bfloat16)
 
     stats_copy(others, others, partner).wait_send()
 

time: 32.7 us -> 32.7 us (level)
  no operation moved by 1% of the time
where the time goes in v6:
time: 32.7 us; the launch traced here: 32.6 us
  Pallas kernels  31.8 us (97%)
  local copies, waits for them, and re-layouts  0.8 us (2%)
    pallas_call x1, Pallas kernels, body(): pl.pallas_call(functools.partial(kernel, n), out_shape=pltpu.VMEM((rows,...  31.8 us
    unnamed x1, local copies, waits for them, and re-layouts  0.8 us

profile of v6, /device:TPU:0, one launch (start us, length us, event | category | flops | bytes accessed | tf_op | source)
XLA Modules:
  0.0 32.6 jit_solution(17687889799143806903)
XLA Ops:
  0.0 31.8 %shard_map.109 = bf16[512,512]{1,0:T(8,128)(2,1)S(1)} custom-call(bf16[512,512]{1,0:T(8,128)(2,1)} %atoms_hbm.1, s32[1,5,512,512]{3,2,1,0:T(8,128)} %mask_hbm.1, f32[1,512]{1,0:T(1,128)} %bitcast.3, bf16[512,512]{1,0:T(8,128)(2,1)} %wq_hbm.1, bf16[512,512]{1,0:T(8,128)(2,1)} %wk_hbm.1, bf16[512,512]{1,0:T(8,128)(2,1)} %wv_hbm.1, bf16[512,512]{1,0:T(8,128)(2,1)} %wo_hbm.1, ...), custom_call_target="tpu_custom_call" | custom-call | tf_op jit(solution)/shard_map/pallas_call | solution.py:382
  31.8 0.8 %copy.13 = bf16[512,512]{1,0:T(8,128)(2,1)} copy(bf16[512,512]{1,0:T(8,128)(2,1)S(1)} %shard_map.109) | data formatting | bytes 1048576
